TPU v7x, 32 devices: a whole 2x2x4 slice. The times are simulated.
32 devices in a mesh: blk: 16 (over z, y, x), rep: 2 (over core).
Axes of the slice: x: 2, y: 2, z: 4, core: 2. Of those that a mesh axis runs over, the one named last changes fastest.
Arguments:
- load_coef: bfloat16 [32, 2049, 256], P('blk', None, 'rep'), parts along dimension 2, may hold values from -0.29882812 to 0.29882812
- legendre: bfloat16 [32, 2049, 1024], P('blk'), may hold values from -0.125 to 0.125
- slab_orders: int32 [32], replicated, may hold values from 0 to 1023, as said below
- cycle_rows: int32 [1024], replicated, may hold values from 0 to 1023, each once
Outputs:
- potential: bfloat16 [1024, 128, 4096], P('blk', 'rep'), parts along dimension 1
- energy: float32 [128], P('rep'), parts along dimension 0
There are 2 independent parts, one for each index of `rep`. A program takes and returns all parts, laid end to end along the dimension named above; an argument that names none is the same for every part. Nothing has to cross between parts.
Inputs may be any that keep to these rules, and one draw needn't show every extreme that they name: `slab_orders`: values are distinct and below (2048) / 2. `cycle_rows`: each cycle appears once.
All inputs are finite; a program needn't handle non-finite values.
Results may differ from a plain program's by a relative error of at most 0.0055.
Values may be sent and summed in bfloat16 or wider, within the bound.
A program may use at most 192 MiB of HBM per device.

v0:
```python
import math
import jax
import jax.numpy as jnp
from jax import lax
from jax.sharding import PartitionSpec as P

NLON = 4096


def basis_rows(frequency):
    coarse_ids = jnp.arange(NLON // 64, dtype=jnp.int32) * 64
    fine_ids = jnp.arange(64, dtype=jnp.int32)
    scale = 2.0 * math.pi / NLON
    coarse_angles = (frequency[:, None] * coarse_ids[None, :] % NLON).astype(jnp.float32) * scale
    fine_angles = (frequency[:, None] * fine_ids[None, :] % NLON).astype(jnp.float32) * scale
    cos_coarse = jnp.cos(coarse_angles)[:, :, None]
    sin_coarse = jnp.sin(coarse_angles)[:, :, None]
    cos_fine = jnp.cos(fine_angles)[:, None, :]
    sin_fine = jnp.sin(fine_angles)[:, None, :]
    cosine = (cos_coarse * cos_fine - sin_coarse * sin_fine).reshape(frequency.shape[0], NLON)
    sine = (sin_coarse * cos_fine + cos_coarse * sin_fine).reshape(frequency.shape[0], NLON)
    factor = jnp.where(frequency == 0, 1.0, 2.0).astype(jnp.float32)[:, None]
    return ((factor * cosine).astype(jnp.bfloat16), (-factor * sine).astype(jnp.bfloat16))


def fourier(received, low_orders, degree):
    cos_lower, sin_lower = basis_rows(low_orders)
    cos_upper, sin_upper = basis_rows(degree - low_orders)
    fourier_basis = jnp.stack([cos_lower, sin_lower, cos_upper, sin_upper], axis=1)
    return jnp.einsum("rnsf,nsk->rfk", received, fourier_basis, preferred_element_type=jnp.float32)


def shards(load_coef, legendre, slab_orders, cycle_rows):
    blocks = lax.axis_size("blk")
    position = lax.axis_index("blk")
    pair_count = load_coef.shape[0]
    slab_rows = load_coef.shape[1]
    fields = load_coef.shape[2] // 2
    lat_count = legendre.shape[2]
    cycle_count = lat_count // blocks
    degree = slab_rows - 2
    my_orders = lax.dynamic_slice_in_dim(slab_orders, position * pair_count, pair_count)
    row_ids = jnp.arange(slab_rows, dtype=jnp.int32)
    spectra = []
    for pair_index in range(pair_count):
        in_lower = (row_ids < slab_rows - 1 - my_orders[pair_index])[:, None]
        pair_coef = load_coef[pair_index]
        nothing = jnp.zeros_like(pair_coef)
        stacked = jnp.concatenate(
            [jnp.where(in_lower, pair_coef, nothing), jnp.where(in_lower, nothing, pair_coef)],
            axis=1,
        )
        spectra.append(
            lax.dot_general(
                legendre[pair_index],
                stacked,
                (((0,), (0,)), ((), ())),
                preferred_element_type=jnp.float32,
            ).astype(jnp.bfloat16)
        )
    spectra = jnp.stack(spectra, axis=1).reshape(lat_count, pair_count, 4, fields)
    spectra = jnp.take(spectra, cycle_rows, axis=0)
    all_orders = slab_orders.reshape(blocks, pair_count)
    cycle_grid = jnp.zeros((cycle_count, fields, NLON), jnp.float32)
    for pair_index in range(pair_count):
        cycle_grid = cycle_grid + fourier(
            lax.all_to_all(
                spectra[:, pair_index : pair_index + 1],
                "blk",
                split_axis=0,
                concat_axis=1,
                tiled=True,
            ),
            low_orders=all_orders[:, pair_index],
            degree=degree,
        )
    partial_energy = jnp.sum(cycle_grid * cycle_grid, axis=(0, 2))
    summed = lax.psum(partial_energy, "blk")
    energy = summed / (lat_count * NLON)
    return (cycle_grid.astype(jnp.bfloat16), energy)


def solution(mesh):
    in_specs = (P("blk", None, "rep"), P("blk", None, None), P(), P())
    out_specs = (P("blk", "rep", None), P("rep"))
    return jax.shard_map(shards, mesh=mesh, in_specs=in_specs, out_specs=out_specs, check_vma=False)
```

profile of v0, /device:TPU:0, one launch (start us, length us, event | category | flops | bytes accessed | tf_op | source)
XLA Modules:
  0.0 187.0 jit_solution(15199914749275640568)
XLA Ops:
  0.6 0.7 compare_and_fusion
  1.3 0.7 fusion.83
  2.0 0.7 dynamic_slice.3
  2.7 0.6 fusion.91
  4.7 3.6 %fusion.90 = (bf16[1,2049,128]{2,0,1:T(2,128)(2,1)S(1)}, bf16[1,2049,128]{2,0,1:T(2,128)(2,1)S(1)}) fusion(bf16[2,2049,128]{2,0,1:T(2,128)(2,1)} %param.4), kind=kLoop, calls=%fused_computation.175 | loop fusion | bytes 2098176 | tf_op jit(solution)/shard_map/slice | solution.py:47
  8.3 17.4 %fusion.88 = (bf16[1,2049,1024]{2,0,1:T(2,128)(2,1)}, bf16[1,2049,1024]{2,0,1:T(2,128)(2,1)S(1)}) fusion(bf16[2,2049,1024]{2,0,1:T(2,128)(2,1)} %param.5), kind=kLoop, calls=%fused_computation.173 | loop fusion | bytes 16785408 | tf_op jit(solution)/shard_map/slice | solution.py:55
  25.7 1.9 %broadcast_select_fusion.2 = (bf16[2049,128]{1,0:T(8,128)(2,1)S(1)}, bf16[2049,128]{1,0:T(8,128)(2,1)S(1)}, bf16[2049,128]{1,0:T(8,128)(2,1)S(1)}, bf16[2049,128]{1,0:T(8,128)(2,1)S(1)}) fusion(pred[2049]{0:T(1024)(128)(4,1)S(1)} %iota_compare_fusion, bf16[1,2049,128]{2,0,1:T(2,128)(2,1)S(1)} %get-tuple-element.25, ...), kind=kLoop, calls=%fused_computation.25 | loop fusion | flops 1049088 | bytes 3151362 | tf_op jit(solution)/shard_map/jit(_where)/select_n | solution.py:50
  27.6 1.5 fusion.3
  29.2 0.7 copy.12
  29.9 4.9 %fusion.2 = bf16[256,1024]{1,0:T(8,128)(2,1)S(1)} fusion(bf16[1,2049,1024]{2,0,1:T(2,128)(2,1)} %get-tuple-element.16, bf16[2049,128]{1,0:T(8,128)(2,1)S(1)} %get-tuple-element.71, bf16[2049,128]{1,0:T(8,128)(2,1)S(1)} %get-tuple-element.72), kind=kOutput, calls=%fused_computation.9 | convolution fusion | flops 1076626432 | bytes 5769728 | tf_op jit(solution)/shard_map/dot_general | solution.py:54
  34.8 0.7 copy.11
  35.5 3.1 %pad_maximum_fusion = bf16[1024,2,4,64]{3,2,1,0:T(4,128)(2,1)} fusion(bf16[1024,1,4,64]{3,2,1,0:T(4,128)(2,1)S(1)} %copy.12, bf16[1024,1,4,64]{3,2,1,0:T(4,128)(2,1)S(1)} %copy.11), kind=kLoop, calls=%fused_computation.7 | loop fusion | flops 524288 | bytes 2097152 | tf_op jit(solution)/shard_map/stack | solution.py:61
  38.6 5.8 %gather_fusion = bf16[1024,2,4,64]{3,2,1,0:T(4,128)(2,1)S(1)} fusion(bf16[1024,2,4,64]{3,2,1,0:T(4,128)(2,1)} %pad_maximum_fusion, s32[1024]{0:T(1024)S(1)} %fusion.83), kind=kCustom, calls=%fused_computation | custom fusion | bytes 2101248 | tf_op jit(solution)/shard_map/jit(_take)/gather | solution.py:62
  44.4 3.8 %broadcast_select_fusion = bf16[1024,2,4,64]{3,2,1,0:T(4,128)(2,1)S(1)} fusion(bf16[1024,2,4,64]{3,2,1,0:T(4,128)(2,1)S(1)} %gather_fusion, pred[1024]{0:T(1024)(128)(4,1)S(1)} %compare_and_fusion), kind=kLoop, calls=%fused_computation.8 | loop fusion | flops 524288 | bytes 2098176 | tf_op jit(solution)/shard_map/jit(_take)/select_n | solution.py:62
  48.3 0.7 fusion.89
  49.0 0.0 copy-start.4
  49.0 1.5 reshape.1147
  50.5 8.3 %all-to-all-start = ((bf16[16,2,8192]{2,1,0:T(2,128)(2,1)}), bf16[16,2,8192]{2,1,0:T(2,128)(2,1)S(1)}, u32[]{:S(2)}, u32[]{:S(2)}) async-start(bf16[16,2,8192]{2,1,0:T(2,128)(2,1)} %reshape.1147), calls=%async_computation | async-start | bytes 1048576 | tf_op jit(solution)/shard_map/all_to_all | solution.py:67
  58.9 0.0 copy-done.4
  58.9 0.1 reshape.1121
  59.0 0.2 slice_reduce_fusion
  59.2 0.1 slice_compare_fusion
  59.3 0.3 fusion.76
  59.6 1.4 multiply_subtract_fusion
  61.0 1.9 %sub.99 = f32[16,1,4096]{2,0,1:T(8,128)} reshape(f32[16,64,64]{2,1,0:T(8,128)} %get-tuple-element.28) | data formatting | bytes 524288 | tf_op jit(solution)/shard_map/sub | solution.py:20
  62.9 0.9 add.180
  63.8 0.9 add.176
  64.7 0.2 sub.95
  64.9 1.4 multiply_subtract_fusion.2
  66.3 1.9 %sub.93 = f32[16,1,4096]{2,0,1:T(8,128)} reshape(f32[16,64,64]{2,1,0:T(8,128)} %get-tuple-element.32) | data formatting | bytes 524288 | tf_op jit(solution)/shard_map/sub | solution.py:20
  68.2 0.9 add.172
  69.1 0.0 copy-start
  69.1 0.2 add.168
  69.3 0.1 select_reduce_fusion
  69.5 0.2 select_reduce_fusion.2
  69.6 1.0 multiply_convert_fusion.1
  70.7 1.7 multiply_convert_fusion
  72.3 1.7 multiply_convert_fusion.2
  74.0 0.7 multiply_convert_fusion.3
  74.7 1.0 multiply_convert_fusion.5
  75.8 0.0 copy-done
  75.8 0.1 multiply_convert_fusion.4
  75.9 0.1 multiply_convert_fusion.6
  76.0 0.2 sub.89
  76.1 1.5 reshape.1149
  77.7 0.1 multiply_convert_fusion.7
  77.7 0.0 all-to-all-done
  77.8 6.9 %all-to-all-start.1 = ((bf16[16,2,8192]{2,1,0:T(2,128)(2,1)}), bf16[16,2,8192]{2,1,0:T(2,128)(2,1)S(1)}, u32[]{:S(2)}, u32[]{:S(2)}) async-start(bf16[16,2,8192]{2,1,0:T(2,128)(2,1)} %reshape.1149), calls=%async_computation.1 | async-start | bytes 1048576 | tf_op jit(solution)/shard_map/all_to_all | solution.py:67
  84.7 0.7 reshape.1148
  85.3 0.0 copy-start.1
  85.3 0.0 copy-start.2
  85.4 0.0 copy-start.3
  85.4 23.2 %fusion.11 = f32[64,64,4096,1]{2,1,3,0:T(8,128)} fusion(bf16[16,64,1,4,64]{4,3,1,0,2:T(4,128)(2,1)S(1)} %bitcast.61, bf16[16,1,4096]{2,0,1:T(8,128)(2,1)S(1)} %multiply_convert_fusion.4, bf16[16,1,4096]{2,0,1:T(8,128)(2,1)S(1)} %multiply_convert_fusion.5, bf16[16,1,4096]{2,0,1:T(8,128)(2,1)S(1)} %multiply_convert_fusion.6, ...), kind=kOutput, calls=%fused_computation.18 | convolution fusion | flops 2148270080 | bytes 68157440 | tf_op jit(solution)/shard_map/rnsf,nsk->rfk/dot_general | solution.py:30
  108.6 0.0 all-to-all-done.1
  108.6 0.7 reshape.1150
  109.2 0.0 copy-done.1
  109.2 0.0 copy-done.2
  109.2 0.0 copy-done.3
  109.3 35.2 %multiply_reduce_fusion = (f32[64]{0:T(128)S(1)}, bf16[64,64,4096]{2,1,0:T(8,128)(2,1)}) fusion(bf16[16,1,4096]{2,0,1:T(8,128)(2,1)S(1)} %copy-done.1, bf16[16,1,4096]{2,0,1:T(8,128)(2,1)S(1)} %multiply_convert_fusion.1, bf16[16,1,4096]{2,0,1:T(8,128)(2,1)S(1)} %copy-done.2, bf16[16,1,4096]{2,0,1:T(8,128)(2,1)S(1)} %copy-done.3, ...), kind=kOutput, calls=%fused_computation.2 | convolution fusion | flops 2215378944 | bytes 101712128 | tf_op jit(solution)/shard_map/rnsf,nsk->rfk/dot_general | solution.py:30
  144.4 42.1 %psum.7 = f32[64]{0:T(128)S(1)} all-reduce(f32[64]{0:T(128)S(1)} %get-tuple-element.14), channel_id=1, replica_groups=mesh['blk'=16,'rep'=2] {'blk'}, use_global_device_ids=true, to_apply=%region_1.2 | all-reduce | flops 64 | bytes 512 | tf_op jit(solution)/shard_map/psum | solution.py:78
  186.5 0.5 broadcast_multiply_fusion
  (3 shorter events, 0.0 us)
Async XLA Ops:
  49.0 9.9 %copy-start.4 = (s32[32]{0:T(128)S(1)}, s32[32]{0:T(128)}, u32[]{:S(2)}) copy-start(s32[32]{0:T(128)} %param.6) | copy-start | bytes 388
  50.5 27.2 %all-to-all-start = ((bf16[16,2,8192]{2,1,0:T(2,128)(2,1)}), bf16[16,2,8192]{2,1,0:T(2,128)(2,1)S(1)}, u32[]{:S(2)}, u32[]{:S(2)}) async-start(bf16[16,2,8192]{2,1,0:T(2,128)(2,1)} %reshape.1147), calls=%async_computation | async-start | bytes 1048576 | tf_op jit(solution)/shard_map/all_to_all | solution.py:67
  69.1 6.7 %copy-start = (f32[16,1,4096]{2,0,1:T(8,128)S(1)}, f32[16,1,4096]{2,0,1:T(8,128)}, u32[]{:S(2)}) copy-start(f32[16,1,4096]{2,0,1:T(8,128)} %add.172) | copy-start | bytes 786436
  77.8 30.8 %all-to-all-start.1 = ((bf16[16,2,8192]{2,1,0:T(2,128)(2,1)}), bf16[16,2,8192]{2,1,0:T(2,128)(2,1)S(1)}, u32[]{:S(2)}, u32[]{:S(2)}) async-start(bf16[16,2,8192]{2,1,0:T(2,128)(2,1)} %reshape.1149), calls=%async_computation.1 | async-start | bytes 1048576 | tf_op jit(solution)/shard_map/all_to_all | solution.py:67
  85.3 23.9 %copy-start.1 = (bf16[16,1,4096]{2,0,1:T(8,128)(2,1)S(1)}, bf16[16,1,4096]{2,0,1:T(8,128)(2,1)}, u32[]{:S(2)}) copy-start(bf16[16,1,4096]{2,0,1:T(8,128)(2,1)} %multiply_convert_fusion) | copy-start | bytes 393220
  85.3 23.9 %copy-start.2 = (bf16[16,1,4096]{2,0,1:T(8,128)(2,1)S(1)}, bf16[16,1,4096]{2,0,1:T(8,128)(2,1)}, u32[]{:S(2)}) copy-start(bf16[16,1,4096]{2,0,1:T(8,128)(2,1)} %multiply_convert_fusion.2) | copy-start | bytes 393220
  85.4 23.9 %copy-start.3 = (bf16[16,1,4096]{2,0,1:T(8,128)(2,1)S(1)}, bf16[16,1,4096]{2,0,1:T(8,128)(2,1)}, u32[]{:S(2)}) copy-start(bf16[16,1,4096]{2,0,1:T(8,128)(2,1)} %multiply_convert_fusion.3) | copy-start | bytes 393220
where the time goes:
time: 188 us; the launch traced here: 187 us
  matrix products  64.8 us (34%)
  blocking collectives  42.1 us (22%)
  local copies, waits for them, and re-layouts  41.8 us (22%)
  other arithmetic  20.9 us (11%)
  starting transfers between devices  15.3 us (8%)
  between operations  2.17 us (1%)
    dot_general x2, matrix products, fourier(): jnp.einsum('rnsf,nsk->rfk', received, fourier_basis, preferred_element_ty...  58.4 us
    psum x1, blocking collectives, shards(): summed = lax.psum(partial_energy, 'blk')  42.1 us
    slice x1, local copies, waits for them, and re-layouts, shards(): legendre[pair_index]  17.4 us
    all_to_all x2, starting transfers between devices, shards(): lax.all_to_all(spectra[:, pair_index:pair_index + 1], 'blk', split_axis=0...  15.3 us
    dot_general x2, matrix products, shards(): lax.dot_general(legendre[pair_index], stacked, (((0,), (0,)), ((), ())),...  6.43 us
    gather x1, local copies, waits for them, and re-layouts, shards(): spectra = jnp.take(spectra, cycle_rows, axis=0)  5.81 us
    unnamed x14, local copies, waits for them, and re-layouts  4.35 us
    sub x4, local copies, waits for them, and re-layouts, basis_rows(): cos_coarse * cos_fine - sin_coarse * sin_fine  4.24 us
  transfers between devices with their start and end apart: 2, of which 0 were waited for; matrix products, arithmetic and copies ran while one was open for 23% of the time, Pallas kernels for 0%

commit v1 on v0

--- a/solution.py
+++ b/solution.py
@@ -64,12 +64,18 @@
     cycle_grid = jnp.zeros((cycle_count, fields, NLON), jnp.float32)
     for pair_index in range(pair_count):
         cycle_grid = cycle_grid + fourier(
-            lax.all_to_all(
-                spectra[:, pair_index : pair_index + 1],
-                "blk",
-                split_axis=0,
-                concat_axis=1,
-                tiled=True,
+            jnp.concatenate(
+                lax.all_to_all(
+                    jnp.stack(
+                        jnp.split(
+                            spectra[:, pair_index : pair_index + 1], lax.axis_size("blk"), axis=0
+                        )
+                    ),
+                    "blk",
+                    0,
+                    0,
+                ),
+                axis=1,
             ),
             low_orders=all_orders[:, pair_index],
             degree=degree,

time: 188 us -> 204 us (1.085)
  waiting for transfers between devices: 0.01 us -> 12.7 us
  blocking collectives: 42.1 us -> 39.1 us
  local copies, waits for them, and re-layouts: 41.8 us -> 44.6 us
  other arithmetic: 20.9 us -> 23.4 us
    all_to_all x2, waiting for transfers between devices: 0.01 us -> 12.7 us  [shards(): lax.all_to_all(jnp.stack(jnp.split(spectra[:, pair_index:pair_index + 1],...]
    psum x1, blocking collectives: 42.1 us -> 39.1 us  [shards(): summed = lax.psum(partial_energy, 'blk')]
    gather x1, local copies, waits for them, and re-layouts: 5.81 us -> 8.55 us  [shards(): spectra = jnp.take(spectra, cycle_rows, axis=0)]
    sub x4, local copies, waits for them, and re-layouts: 4.24 us -> 2.13 us  [basis_rows(): cos_coarse * cos_fine - sin_coarse * sin_fine]
    unnamed x14 -> x74, local copies, waits for them, and re-layouts: 4.35 us -> 6.22 us
  transfers between devices with their start and end apart: 2 -> 2, of which waited for: 0 -> 1; matrix products, arithmetic and copies ran while one was open for 23% -> 10% of each run, Pallas kernels for 0% -> 0%
where the time goes in v1:
time: 204 us; the launch traced here: 203 us
  matrix products  65.6 us (32%)
  local copies, waits for them, and re-layouts  44.6 us (22%)
  blocking collectives  39.1 us (19%)
  other arithmetic  23.4 us (11%)
  starting transfers between devices  15.3 us (8%)
  waiting for transfers between devices  12.7 us (6%)
  between operations  2.47 us (1%)
    dot_general x2, matrix products, fourier(): jnp.einsum('rnsf,nsk->rfk', received, fourier_basis, preferred_element_ty...  59.1 us
    psum x1, blocking collectives, shards(): summed = lax.psum(partial_energy, 'blk')  39.1 us
    slice x1, local copies, waits for them, and re-layouts, shards(): legendre[pair_index]  17.4 us
    all_to_all x2, starting transfers between devices, shards(): lax.all_to_all(jnp.stack(jnp.split(spectra[:, pair_index:pair_index + 1],...  15.3 us
    all_to_all x2, waiting for transfers between devices, shards(): lax.all_to_all(jnp.stack(jnp.split(spectra[:, pair_index:pair_index + 1],...  12.7 us
    gather x1, local copies, waits for them, and re-layouts, shards(): spectra = jnp.take(spectra, cycle_rows, axis=0)  8.55 us
    dot_general x2, matrix products, shards(): lax.dot_general(legendre[pair_index], stacked, (((0,), (0,)), ((), ())),...  6.43 us
    unnamed x74, local copies, waits for them, and re-layouts  6.22 us
  transfers between devices with their start and end apart: 2, of which 1 were waited for; matrix products, arithmetic and copies ran while one was open for 10% of the time, Pallas kernels for 0%

profile of v1, /device:TPU:0, one launch (start us, length us, event | category | flops | bytes accessed | tf_op | source)
XLA Modules:
  0.0 203.2 jit_solution(15300780508807899598)
XLA Ops:
  0.6 0.7 compare_and_fusion
  1.3 0.7 fusion.99
  2.0 0.7 dynamic_slice.3
  2.7 0.6 fusion.107
  4.7 3.6 %fusion.106 = (bf16[1,2049,128]{2,0,1:T(2,128)(2,1)S(1)}, bf16[1,2049,128]{2,0,1:T(2,128)(2,1)S(1)}) fusion(bf16[2,2049,128]{2,0,1:T(2,128)(2,1)} %param.4), kind=kLoop, calls=%fused_computation.222 | loop fusion | bytes 2098176 | tf_op jit(solution)/shard_map/slice | solution.py:47
  8.3 17.4 %fusion.104 = (bf16[1,2049,1024]{2,0,1:T(2,128)(2,1)}, bf16[1,2049,1024]{2,0,1:T(2,128)(2,1)S(1)}) fusion(bf16[2,2049,1024]{2,0,1:T(2,128)(2,1)} %param.5), kind=kLoop, calls=%fused_computation.220 | loop fusion | bytes 16785408 | tf_op jit(solution)/shard_map/slice | solution.py:55
  25.7 1.9 bitcast_select_fusion.1
  27.6 1.5 fusion.3
  29.2 0.7 copy.1407
  29.9 4.9 %fusion.2 = bf16[256,1024]{1,0:T(8,128)(2,1)S(1)} fusion(bf16[1,2049,1024]{2,0,1:T(2,128)(2,1)} %get-tuple-element.16, bf16[2049,128]{1,0:T(8,128)(2,1)S(1)} %get-tuple-element.35, bf16[2049,128]{1,0:T(8,128)(2,1)S(1)} %get-tuple-element.34), kind=kOutput, calls=%fused_computation.9 | convolution fusion | flops 1076626432 | bytes 5769728 | tf_op jit(solution)/shard_map/dot_general | solution.py:54
  34.8 1.4 copy.1406
  36.2 3.0 %pad_maximum_fusion = bf16[1024,2,4,64]{3,2,1,0:T(4,128)(2,1)S(1)} fusion(bf16[1024,1,4,64]{3,2,1,0:T(4,128)(2,1)S(1)} %copy.1407, bf16[1024,1,4,64]{3,2,1,0:T(4,128)(2,1)} %copy.1406), kind=kLoop, calls=%fused_computation.7 | loop fusion | flops 524288 | bytes 2097152 | tf_op jit(solution)/shard_map/stack | solution.py:61
  39.2 8.6 %gather_fusion = bf16[1024,2,4,64]{3,2,1,0:T(4,128)(2,1)} fusion(bf16[1024,2,4,64]{3,2,1,0:T(4,128)(2,1)S(1)} %pad_maximum_fusion, s32[1024]{0:T(1024)S(1)} %fusion.99), kind=kCustom, calls=%fused_computation | custom fusion | bytes 2101248 | tf_op jit(solution)/shard_map/jit(_take)/gather | solution.py:62
  47.8 5.2 %broadcast_select_fusion = bf16[1024,2,4,64]{3,2,1,0:T(4,128)(2,1)S(1)} fusion(bf16[1024,2,4,64]{3,2,1,0:T(4,128)(2,1)} %gather_fusion, pred[1024]{0:T(1024)(128)(4,1)S(1)} %compare_and_fusion), kind=kLoop, calls=%fused_computation.8 | loop fusion | flops 524288 | bytes 2098176 | tf_op jit(solution)/shard_map/jit(_take)/select_n | solution.py:62
  53.2 0.0 copy-start.19
  53.7 1.5 reshape.1165
  55.2 8.3 %all-to-all-start.1 = ((bf16[16,2,8192]{2,1,0:T(2,128)(2,1)}), bf16[16,2,8192]{2,1,0:T(2,128)(2,1)S(1)}, u32[]{:S(2)}, u32[]{:S(2)}) async-start(bf16[16,2,8192]{2,1,0:T(2,128)(2,1)} %reshape.1165), calls=%async_computation.1 | async-start | bytes 1048576 | tf_op jit(solution)/shard_map/all_to_all | solution.py:68
  63.5 0.0 copy-done.19
  63.5 0.1 reshape.1135
  63.6 0.2 slice_reduce_fusion
  63.8 0.7 slice_compare_fusion
  64.5 1.2 fusion.105
  65.8 1.0 fusion.92
  66.7 0.6 multiply_subtract_fusion
  67.3 0.9 sub.99
  68.2 0.2 add.180
  68.4 0.2 add.176
  68.6 0.2 sub.95
  68.8 1.4 multiply_subtract_fusion.2
  70.2 0.9 sub.93
  71.1 0.9 add.172
  72.0 0.0 copy-start.15
  72.0 0.0 copy-start.14
  72.1 1.0 constant_dynamic-update-slice_fusion.15
  73.0 0.8 select_reduce_fusion
  73.9 0.8 select_reduce_fusion.2
  74.7 1.7 multiply_convert_fusion.1
  76.4 0.7 multiply_convert_fusion
  77.1 0.7 multiply_convert_fusion.2
  77.8 0.7 multiply_convert_fusion.3
  78.6 1.0 multiply_convert_fusion.5
  79.6 0.1 multiply_convert_fusion.4
  79.9 0.0 copy-done.11
  80.0 0.0 copy-done.9
  80.1 0.0 copy-done.7
  80.2 0.2 add.168
  80.4 0.2 sub.89
  80.6 1.5 reshape.1163
  82.1 0.1 multiply_convert_fusion.6
  82.2 0.0 all-to-all-done.1
  82.2 6.9 %all-to-all-start = ((bf16[16,2,8192]{2,1,0:T(2,128)(2,1)}), bf16[16,2,8192]{2,1,0:T(2,128)(2,1)S(1)}, u32[]{:S(2)}, u32[]{:S(2)}) async-start(bf16[16,2,8192]{2,1,0:T(2,128)(2,1)} %reshape.1163), calls=%async_computation | async-start | bytes 1048576 | tf_op jit(solution)/shard_map/all_to_all | solution.py:68
  89.1 0.7 multiply_convert_fusion.7
  89.9 0.7 reshape.1166
  90.5 0.4 bitcast_bitcast_fusion
  90.9 0.0 copy-start.1
  90.9 12.7 %all-to-all-done = bf16[16,2,8192]{2,1,0:T(2,128)(2,1)S(1)} async-done(((bf16[16,2,8192]{2,1,0:T(2,128)(2,1)}), bf16[16,2,8192]{2,1,0:T(2,128)(2,1)S(1)}, u32[]{:S(2)}, u32[]{:S(2)}) %all-to-all-start) | async-done | bytes 524320 | tf_op jit(solution)/shard_map/all_to_all | solution.py:68
  103.6 0.7 reshape.1164
  104.3 0.1 bitcast_bitcast_fusion.1
  104.4 24.0 %fusion.11 = f32[64,64,4096,1]{2,1,3,0:T(8,128)} fusion(bf16[64,16,1,4,64]{4,0,3,2,1:T(8,128)(2,1)S(1)} %bitcast_bitcast_fusion.1, bf16[16,1,4096]{2,0,1:T(8,128)(2,1)S(1)} %multiply_convert_fusion.4, bf16[16,1,4096]{2,0,1:T(8,128)(2,1)S(1)} %multiply_convert_fusion.5, bf16[16,1,4096]{2,0,1:T(8,128)(2,1)S(1)} %multiply_convert_fusion.6, ...), kind=kOutput, calls=%fused_computation.18 | convolution fusion | flops 2148270080 | bytes 68157440 | tf_op jit(solution)/shard_map/rnsf,nsk->rfk/dot_general | solution.py:30
  128.4 0.0 copy-done.2
  128.4 0.0 copy-done.4
  128.4 35.2 %multiply_reduce_fusion = (f32[64]{0:T(128)S(1)}, bf16[64,64,4096]{2,1,0:T(8,128)(2,1)}) fusion(bf16[16,1,4096]{2,0,1:T(8,128)(2,1)S(1)} %copy-done.3, bf16[16,1,4096]{2,0,1:T(8,128)(2,1)S(1)} %copy-done.2, bf16[16,1,4096]{2,0,1:T(8,128)(2,1)S(1)} %copy-done.4, bf16[16,1,4096]{2,0,1:T(8,128)(2,1)S(1)} %copy-done.5, ...), kind=kOutput, calls=%fused_computation.2 | convolution fusion | flops 2215378944 | bytes 101712128 | tf_op jit(solution)/shard_map/rnsf,nsk->rfk/dot_general | solution.py:30
  163.6 39.1 %psum.7 = f32[64]{0:T(128)S(1)} all-reduce(f32[64]{0:T(128)S(1)} %get-tuple-element.14), channel_id=1, replica_groups=mesh['blk'=16,'rep'=2] {'blk'}, use_global_device_ids=true, to_apply=%region_1.2 | all-reduce | flops 64 | bytes 512 | tf_op jit(solution)/shard_map/psum | solution.py:84
  202.7 0.5 broadcast_multiply_fusion
  (64 shorter events, 1.0 us)
Async XLA Ops:
  53.2 10.4 %copy-start.19 = (s32[32]{0:T(128)S(1)}, s32[32]{0:T(128)}, u32[]{:S(2)}) copy-start(s32[32]{0:T(128)} %param.6) | copy-start | bytes 388
  55.2 27.0 %all-to-all-start.1 = ((bf16[16,2,8192]{2,1,0:T(2,128)(2,1)}), bf16[16,2,8192]{2,1,0:T(2,128)(2,1)S(1)}, u32[]{:S(2)}, u32[]{:S(2)}) async-start(bf16[16,2,8192]{2,1,0:T(2,128)(2,1)} %reshape.1165), calls=%async_computation.1 | async-start | bytes 1048576 | tf_op jit(solution)/shard_map/all_to_all | solution.py:68
  72.0 7.6 %copy-start = (f32[16,1,4096]{2,0,1:T(8,128)S(1)}, f32[16,1,4096]{2,0,1:T(8,128)}, u32[]{:S(2)}) copy-start(f32[16,1,4096]{2,0,1:T(8,128)} %add.172) | copy-start | bytes 786436
  72.0 7.7 %copy-start.18 = (bf16[64,1,4,64]{3,2,1,0:T(4,128)(2,1)S(1)}, bf16[64,1,4,64]{3,2,1,0:T(4,128)(2,1)}, u32[]{:S(2)}) copy-start(bf16[64,1,4,64]{3,2,1,0:T(4,128)(2,1)} %get-tuple-element.32) | copy-start | bytes 98308
  72.0 7.8 %copy-start.17 = (bf16[64,1,4,64]{3,2,1,0:T(4,128)(2,1)S(1)}, bf16[64,1,4,64]{3,2,1,0:T(4,128)(2,1)}, u32[]{:S(2)}) copy-start(bf16[64,1,4,64]{3,2,1,0:T(4,128)(2,1)} %get-tuple-element.31) | copy-start | bytes 98308
  72.0 7.8 %copy-start.16 = (bf16[64,1,4,64]{3,2,1,0:T(4,128)(2,1)S(1)}, bf16[64,1,4,64]{3,2,1,0:T(4,128)(2,1)}, u32[]{:S(2)}) copy-start(bf16[64,1,4,64]{3,2,1,0:T(4,128)(2,1)} %get-tuple-element.30) | copy-start | bytes 98308
  72.0 7.8 %copy-start.15 = (bf16[64,1,4,64]{3,2,1,0:T(4,128)(2,1)S(1)}, bf16[64,1,4,64]{3,2,1,0:T(4,128)(2,1)}, u32[]{:S(2)}) copy-start(bf16[64,1,4,64]{3,2,1,0:T(4,128)(2,1)} %get-tuple-element.29) | copy-start | bytes 98308
  72.0 7.9 %copy-start.14 = (bf16[64,1,4,64]{3,2,1,0:T(4,128)(2,1)S(1)}, bf16[64,1,4,64]{3,2,1,0:T(4,128)(2,1)}, u32[]{:S(2)}) copy-start(bf16[64,1,4,64]{3,2,1,0:T(4,128)(2,1)} %get-tuple-element.28) | copy-start | bytes 98308
  72.0 7.9 %copy-start.13 = (bf16[64,1,4,64]{3,2,1,0:T(4,128)(2,1)S(1)}, bf16[64,1,4,64]{3,2,1,0:T(4,128)(2,1)}, u32[]{:S(2)}) copy-start(bf16[64,1,4,64]{3,2,1,0:T(4,128)(2,1)} %get-tuple-element.27) | copy-start | bytes 98308
  72.0 7.9 %copy-start.12 = (bf16[64,1,4,64]{3,2,1,0:T(4,128)(2,1)S(1)}, bf16[64,1,4,64]{3,2,1,0:T(4,128)(2,1)}, u32[]{:S(2)}) copy-start(bf16[64,1,4,64]{3,2,1,0:T(4,128)(2,1)} %get-tuple-element.26) | copy-start | bytes 98308
  72.0 7.9 %copy-start.11 = (bf16[64,1,4,64]{3,2,1,0:T(4,128)(2,1)S(1)}, bf16[64,1,4,64]{3,2,1,0:T(4,128)(2,1)}, u32[]{:S(2)}) copy-start(bf16[64,1,4,64]{3,2,1,0:T(4,128)(2,1)} %get-tuple-element.25) | copy-start | bytes 98308
  72.0 8.0 %copy-start.10 = (bf16[64,1,4,64]{3,2,1,0:T(4,128)(2,1)S(1)}, bf16[64,1,4,64]{3,2,1,0:T(4,128)(2,1)}, u32[]{:S(2)}) copy-start(bf16[64,1,4,64]{3,2,1,0:T(4,128)(2,1)} %get-tuple-element.24) | copy-start | bytes 98308
  72.0 8.0 %copy-start.9 = (bf16[64,1,4,64]{3,2,1,0:T(4,128)(2,1)S(1)}, bf16[64,1,4,64]{3,2,1,0:T(4,128)(2,1)}, u32[]{:S(2)}) copy-start(bf16[64,1,4,64]{3,2,1,0:T(4,128)(2,1)} %get-tuple-element.23) | copy-start | bytes 98308
  72.0 8.0 %copy-start.8 = (bf16[64,1,4,64]{3,2,1,0:T(4,128)(2,1)S(1)}, bf16[64,1,4,64]{3,2,1,0:T(4,128)(2,1)}, u32[]{:S(2)}) copy-start(bf16[64,1,4,64]{3,2,1,0:T(4,128)(2,1)} %get-tuple-element.22) | copy-start | bytes 98308
  72.1 8.0 %copy-start.7 = (bf16[64,1,4,64]{3,2,1,0:T(4,128)(2,1)S(1)}, bf16[64,1,4,64]{3,2,1,0:T(4,128)(2,1)}, u32[]{:S(2)}) copy-start(bf16[64,1,4,64]{3,2,1,0:T(4,128)(2,1)} %get-tuple-element.21) | copy-start | bytes 98308
  72.1 8.1 %copy-start.6 = (bf16[64,1,4,64]{3,2,1,0:T(4,128)(2,1)S(1)}, bf16[64,1,4,64]{3,2,1,0:T(4,128)(2,1)}, u32[]{:S(2)}) copy-start(bf16[64,1,4,64]{3,2,1,0:T(4,128)(2,1)} %get-tuple-element.20) | copy-start | bytes 98308
  82.2 21.4 %all-to-all-start = ((bf16[16,2,8192]{2,1,0:T(2,128)(2,1)}), bf16[16,2,8192]{2,1,0:T(2,128)(2,1)S(1)}, u32[]{:S(2)}, u32[]{:S(2)}) async-start(bf16[16,2,8192]{2,1,0:T(2,128)(2,1)} %reshape.1163), calls=%async_computation | async-start | bytes 1048576 | tf_op jit(solution)/shard_map/all_to_all | solution.py:68
  90.9 13.5 %copy-start.1 = (bf16[16,1,4096]{2,0,1:T(8,128)(2,1)S(1)}, bf16[16,1,4096]{2,0,1:T(8,128)(2,1)}, u32[]{:S(2)}) copy-start(bf16[16,1,4096]{2,0,1:T(8,128)(2,1)} %multiply_convert_fusion.7) | copy-start | bytes 393220
  104.4 24.0 %copy-start.2 = (bf16[16,1,4096]{2,0,1:T(8,128)(2,1)S(1)}, bf16[16,1,4096]{2,0,1:T(8,128)(2,1)}, u32[]{:S(2)}) copy-start(bf16[16,1,4096]{2,0,1:T(8,128)(2,1)} %multiply_convert_fusion.1) | copy-start | bytes 393220
  104.4 24.0 %copy-start.3 = (bf16[16,1,4096]{2,0,1:T(8,128)(2,1)S(1)}, bf16[16,1,4096]{2,0,1:T(8,128)(2,1)}, u32[]{:S(2)}) copy-start(bf16[16,1,4096]{2,0,1:T(8,128)(2,1)} %multiply_convert_fusion) | copy-start | bytes 393220
  104.4 24.0 %copy-start.4 = (bf16[16,1,4096]{2,0,1:T(8,128)(2,1)S(1)}, bf16[16,1,4096]{2,0,1:T(8,128)(2,1)}, u32[]{:S(2)}) copy-start(bf16[16,1,4096]{2,0,1:T(8,128)(2,1)} %multiply_convert_fusion.2) | copy-start | bytes 393220
  104.4 24.0 %copy-start.5 = (bf16[16,1,4096]{2,0,1:T(8,128)(2,1)S(1)}, bf16[16,1,4096]{2,0,1:T(8,128)(2,1)}, u32[]{:S(2)}) copy-start(bf16[16,1,4096]{2,0,1:T(8,128)(2,1)} %multiply_convert_fusion.3) | copy-start | bytes 393220
